TPU v7x, 128 devices: a whole 4x4x4 slice. The times are simulated.
128 devices in a mesh: row: 8 (over z, core), col: 16 (over x, y).
Axes of the slice: x: 4, y: 4, z: 4, core: 2. Of those that a mesh axis runs over, the one named last changes fastest.
Arguments:
- edge_code: int32 [128, 4096], P(('row', 'col')), may hold values from 0 to 1572863
- edge_weight: bfloat16 [128, 4096], P(('row', 'col')), may hold values from 1 to 64
- edge_count: int32 [128, 128], P(('row', 'col')), may hold values from 0 to 32, as said below
- tile_blocks: int32 [128, 4, 2], P(('row', 'col')), may hold values from 0 to 127
- hub_blocks: int32 [8, 2, 2], P('row'), may hold values from 0 to 127
- node_degree: float32 [128, 512], P(('row', 'col')), may hold values from 1 to 16
Outputs:
- owned_tiles: float32 [512, 512, 512], P(('row', 'col'))
- hub_tiles: float32 [8192, 512], P(('row', 'col'))
Inputs may be any that keep to these rules, and one draw needn't show every extreme that they name: `edge_count`: at most 32 used slots from one device to another; in every draw some device receives 32 used slots from every device, and the loads of destinations differ widely.
All inputs are finite; a program needn't handle non-finite values.
Results may differ from a plain program's by a relative error of at most 0.0003.
Values may be sent and summed in bfloat16 or wider, within the bound.
A program may use at most 64 MiB of HBM per device.

v0:
```python
import jax
import jax.numpy as jnp
from jax import lax
from jax.sharding import Mesh
from jax.sharding import PartitionSpec as P

TILE = 512
TILES_DEV = 4
HUBS = 2
CAP = 32
ROW = ("row_0", "row_1")
COL = ("col_0", "col_1")
ROW_COL = ("row_0", "row_1", "col_0", "col_1")


def cut_along(x, dim, size):
    before, after = (x.shape[:dim], x.shape[dim + 1 :])
    return jnp.moveaxis(x.reshape(*before, size, -1, *after), dim, 0)


def in_order(blocks, dim):
    blocks = jnp.moveaxis(blocks, 0, dim)
    dims = blocks.shape
    return blocks.reshape(*dims[:dim], dims[dim] * dims[dim + 1], *dims[dim + 2 :])


def one_exchange(x, axis, axes, splits, concats):
    sizes = [lax.axis_size(a) for a in axes]
    blocks = cut_along(x, splits[0], sizes[0])
    blocks = jnp.moveaxis(cut_along(blocks, splits[1] + 1, sizes[1]), 0, 1)
    inside = blocks.shape[2:]
    blocks = blocks.reshape(-1, *inside)
    blocks = lax.all_to_all(blocks, axis, split_axis=0, concat_axis=0, tiled=True)
    blocks = in_order(blocks.reshape(*sizes, *inside), concats[0] + 1)
    return in_order(blocks, concats[1])


def stacked_from(x, axes, order):
    blocks = x[None]
    for k in order:
        blocks = lax.all_gather(blocks, axes[k], axis=0, tiled=True)
    block = [lax.axis_size(axes[k]) for k in reversed(order)]
    blocks = blocks.reshape(*block, *x.shape)
    turned = sorted(range(len(order)), key=lambda place: order[len(order) - 1 - place])
    return blocks.transpose(*turned, *range(len(order), blocks.ndim)).reshape(-1, *x.shape)


def gather_axes(x, axes, order, dim):
    return in_order(stacked_from(x, axes, order), dim)


def sum_at_owner(x, axis, dim):
    size = lax.axis_size(axis)
    blocks = lax.all_to_all(cut_along(x, dim, size), axis, 0, 0, tiled=True)
    return jnp.sum(blocks.astype(jnp.float32), axis=0)


def lookup(indices, degrees):
    selector = (indices[:, None] == jnp.arange(degrees.shape[0], dtype=jnp.int32)[None, :]).astype(
        jnp.float32
    )
    return jnp.dot(selector, degrees, precision=lax.Precision.HIGHEST)


def accumulate_rows(edge_codes, weights, row_count):
    total_edges = edge_codes.shape[0]
    block = 512
    row_keys = jnp.arange(row_count, dtype=jnp.int32)
    col_keys = jnp.arange(TILE, dtype=jnp.int32)

    def step_block(turn, totals):
        start = turn * block
        part_codes = lax.dynamic_slice_in_dim(edge_codes, start, block)
        part_weights = lax.dynamic_slice_in_dim(weights, start, block)
        left_side = jnp.where(
            part_codes[:, None] // TILE == row_keys[None, :],
            part_weights[:, None],
            jnp.zeros((), jnp.bfloat16),
        )
        right_side = (part_codes[:, None] % TILE == col_keys[None, :]).astype(jnp.bfloat16)
        return totals + lax.dot_general(
            left_side, right_side, (((0,), (0,)), ((), ())), preferred_element_type=jnp.float32
        )

    return lax.fori_loop(
        0, total_edges // block, step_block, jnp.zeros((row_count, TILE), jnp.float32)
    )


def shards(edge_code, edge_weight, edge_count, tile_blocks, hub_blocks, node_degree):
    n_row = lax.axis_size(ROW)
    n_col = lax.axis_size(COL)
    devices = n_row * n_col
    edge_codes, weights, counts = (
        one_exchange(edge_code.reshape(n_row, n_col, CAP), ROW_COL, (ROW, COL), (0, 1), (0, 1)),
        one_exchange(edge_weight.reshape(n_row, n_col, CAP), ROW_COL, (ROW, COL), (0, 1), (0, 1)),
        one_exchange(edge_count.reshape(n_row, n_col, 1), ROW_COL, (ROW, COL), (0, 1), (0, 1)),
    )
    edge_codes = edge_codes.reshape(devices, CAP)
    weights = weights.reshape(devices, CAP)
    counts = counts.reshape(devices, 1)
    usable = jnp.arange(CAP, dtype=jnp.int32)[None, :] < counts
    weights = jnp.where(usable, weights, jnp.zeros((), jnp.bfloat16)).reshape(-1)
    edge_codes = edge_codes.reshape(-1)
    degrees = gather_axes(node_degree, ROW_COL, (0, 2, 3, 1), 0)
    scaling = jnp.sum(degrees) / degrees.size
    slab_rows = HUBS * TILE // n_col
    offset = lax.axis_index(COL) * slab_rows
    totals = accumulate_rows(edge_codes, weights, (TILES_DEV + HUBS) * TILE)
    owned = totals[: TILES_DEV * TILE].reshape(TILES_DEV, TILE, TILE)
    summed = sum_at_owner(totals[TILES_DEV * TILE :].astype(jnp.bfloat16), COL, 0)
    blocks = tile_blocks[0]
    row_degree = lookup(blocks[:, 0], degrees)
    col_degree = lookup(blocks[:, 1], degrees)
    owned_tiles = jnp.log(
        jnp.maximum(scaling * owned / (row_degree[:, :, None] * col_degree[:, None, :]), 1.0)
    )
    hub_rows = lookup(hub_blocks[0][:, 0], degrees).reshape(-1)
    hub_row_degree = lax.dynamic_slice_in_dim(hub_rows, offset, slab_rows)
    hub_cols = lookup(hub_blocks[0][:, 1], degrees)
    hub_index = (offset + jnp.arange(slab_rows, dtype=jnp.int32)) // TILE
    selector = (hub_index[:, None] == jnp.arange(HUBS, dtype=jnp.int32)[None, :]).astype(
        jnp.float32
    )
    hub_col_degree = jnp.dot(selector, hub_cols, precision=lax.Precision.HIGHEST)
    hub_tiles = jnp.log(
        jnp.maximum(scaling * summed / (hub_row_degree[:, None] * hub_col_degree), 1.0)
    )
    return (owned_tiles, hub_tiles)


def solution(mesh):
    split = Mesh(mesh.devices.reshape(4, 2, 4, 4), ("row_0", "row_1", "col_0", "col_1"))
    placed = (
        P(ROW_COL, None),
        P(ROW_COL, None),
        P(ROW_COL, None),
        P(ROW_COL, None, None),
        P(ROW, None, None),
        P(ROW_COL, None),
    )
    return jax.shard_map(
        shards,
        mesh=split,
        in_specs=placed,
        out_specs=(P(ROW_COL, None, None), P(ROW_COL, None)),
        check_vma=False,
    )
```

profile of v0, /device:TPU:0, one launch (start us, length us, event | category | flops | bytes accessed | tf_op | source)
XLA Modules:
  0.0 174.7 jit_solution(8583765645140113446)
XLA Ops:
  0.6 1.4 copy.16
  2.0 11.2 %all-to-all-start.1 = ((s32[128,1,1,1]{3,2,1,0:T(1,128)}), s32[128,1,1,1]{3,2,1,0:T(1,128)S(1)}, u32[]{:S(2)}, u32[]{:S(2)}) async-start(s32[128,1,1,1]{3,2,1,0:T(1,128)} %copy.16), calls=%async_computation.1 | async-start | bytes 131072 | tf_op jit(solution)/shard_map/all_to_all | solution.py:33
  13.2 0.8 slice_bitcast_fusion.1
  14.0 1.0 slice_reduce_fusion.1
  15.0 11.1 %all-gather.4 = f32[4,1,512]{2,1,0:T(1,128)S(1)} all-gather(f32[1,1,512]{2,1,0:T(1,128)} %bitcast.64), channel_id=2, replica_groups=mesh['row_0'=4,'row_1'=2,'col_0'=4,'col_1'=4] {'row_0'}, dimensions={0}, use_global_device_ids=true | all-gather | bytes 10240 | tf_op jit(solution)/shard_map/all_gather | solution.py:41
  26.1 12.2 %all-gather.5 = f32[4,4,512]{2,1,0:T(4,128)S(1)} all-gather(f32[1,4,512]{2,1,0:T(4,128)S(1)} %copy.14), channel_id=3, replica_groups=mesh['row_0'=4,'row_1'=2,'col_0'=4,'col_1'=4] {'col_0'}, dimensions={0}, use_global_device_ids=true | all-gather | bytes 40960 | tf_op jit(solution)/shard_map/all_gather | solution.py:41
  38.3 0.5 broadcast.148
  38.9 1.4 reduce.13
  40.3 0.7 reshape_transpose_transpose_reshape_reshape_reshape.9
  41.0 12.4 %all-gather.2 = f32[64,512]{1,0:T(8,128)S(1)} all-gather(f32[16,512]{1,0:T(8,128)S(1)} %reshape.108), channel_id=4, replica_groups=mesh['row_0'=4,'row_1'=2,'col_0'=4,'col_1'=4] {'col_1'}, dimensions={0}, use_global_device_ids=true | all-gather | bytes 163840 | tf_op jit(solution)/shard_map/all_gather | solution.py:41
  53.4 2.0 %all-gather.3 = f32[128,512]{1,0:T(8,128)S(1)} all-gather(f32[64,512]{1,0:T(8,128)S(1)} %all-gather.2), channel_id=5, replica_groups=mesh['row_0'=4,'row_1'=2,'col_0'=4,'col_1'=4] {'row_1'}, dimensions={0}, use_global_device_ids=true | all-gather | bytes 393216 | tf_op jit(solution)/shard_map/all_gather | solution.py:41
  55.4 0.2 copy.22
  55.6 0.1 reshape_reshape.8
  55.7 0.2 fusion.18
  55.9 0.2 convolution_bitcast_fusion
  56.1 0.2 fusion.17
  56.4 0.2 fusion.16
  56.6 0.8 reduce.6
  57.4 0.7 reshape_transpose_transpose_reshape_reshape_reshape.12
  58.1 0.7 reduce_sum.18
  59.5 0.1 dynamic_slice.23
  59.6 7.7 %all-to-all-start.2 = ((bf16[128,1,1,32]{3,2,1,0:T(2,128)(2,1)}), bf16[128,1,1,32]{3,2,1,0:T(2,128)(2,1)S(1)}, u32[]{:S(2)}, u32[]{:S(2)}) async-start(bf16[128,1,1,32]{3,2,1,0:T(2,128)(2,1)} %reshape_transpose_transpose_reshape_reshape_reshape.12), calls=%async_computation.2 | async-start | bytes 131072 | tf_op jit(solution)/shard_map/all_to_all | solution.py:33
  67.3 2.4 %reduce.5 = s32[128]{0:T(128)S(1)} reduce(s32[128,1,1,1]{3,2,1,0:T(1,128)S(1)} %all-to-all-done.1, s32[]{:T(128)} %constant.122.clone.1), dimensions={1,2,3}, to_apply=%all_to_all.13.reduce_sub_computation | reduce | bytes 1028 | tf_op jit(solution)/shard_map/all_to_all | solution.py:33
  69.7 0.1 reshape.93
  69.8 0.1 lt.51
  69.8 0.1 iota_compare_fusion.3
  69.9 0.1 lt.54
  70.0 6.8 %all-to-all-done.2 = bf16[128,1,1,32]{3,2,1,0:T(2,128)(2,1)S(1)} async-done(((bf16[128,1,1,32]{3,2,1,0:T(2,128)(2,1)}), bf16[128,1,1,32]{3,2,1,0:T(2,128)(2,1)S(1)}, u32[]{:S(2)}, u32[]{:S(2)}) %all-to-all-start.2) | async-done | bytes 8224 | tf_op jit(solution)/shard_map/all_to_all | solution.py:33
  76.8 4.6 %all-to-all-start = ((s32[128,1,1,32]{3,2,1,0:T(1,128)}), s32[128,1,1,32]{3,2,1,0:T(1,128)S(1)}, u32[]{:S(2)}, u32[]{:S(2)}) async-start(s32[128,1,1,32]{3,2,1,0:T(1,128)} %bitcast.2), calls=%async_computation | async-start | bytes 131072 | tf_op jit(solution)/shard_map/all_to_all | solution.py:33
  81.4 0.1 reshape_reshape.7
  81.5 9.3 %all-to-all-done = s32[128,1,1,32]{3,2,1,0:T(1,128)S(1)} async-done(((s32[128,1,1,32]{3,2,1,0:T(1,128)}), s32[128,1,1,32]{3,2,1,0:T(1,128)S(1)}, u32[]{:S(2)}, u32[]{:S(2)}) %all-to-all-start) | async-done | bytes 16416 | tf_op jit(solution)/shard_map/all_to_all | solution.py:33
  90.9 0.1 reshape_reshape_reshape.3
  90.9 58.6 %while.16 = (s32[]{:T(128)}, f32[3072,512]{1,0:T(8,128)}, s32[4096]{0:T(1024)S(1)}, bf16[4096]{0:T(1024)(128)(2,1)S(1)}, s32[]{:T(128)}, /*index=5*/s32[]{:T(128)}, s32[]{:T(128)}, s32[]{:T(128)}) while((s32[]{:T(128)}, f32[3072,512]{1,0:T(8,128)}, s32[4096]{0:T(1024)S(1)}, bf16[4096]{0:T(1024)(128)(2,1)S(1)}, s32[]{:T(128)}, ...), condition=%wide.region_2.3_spmd.clone, body=%wide.region_1.2_spmd.clone.sunk | while | flops 1617176064 | bytes 12596381 | solution.py:85
  91.0 0.1 dynamic_slice.35
  91.0 0.1 add_select_fusion.3
  91.1 4.7 %select_add_fusion.2 = f32[3072,512]{1,0:T(8,128)} fusion(f32[3072,512]{1,0:T(8,128)} %get-tuple-element.231, s32[512]{0:T(512)S(1)} %get-tuple-element.220, pred[]{:T(512)S(6)} %compare.23, bf16[512]{0:T(512)(128)(2,1)S(1)} %dynamic_slice.35, s32[512]{0:T(512)S(1)} %get-tuple-element.221), kind=kOutput, calls=%fused_computation.3.clone.1 | convolution fusion | flops 1617166336 | bytes 12588033 | tf_op jit(solution)/shard_map/while/body/eval_jaxpr/dot_general | solution.py:81
  95.9 0.1 dynamic_slice.35
  95.9 0.1 add_select_fusion.3
  96.0 7.5 %select_add_fusion.2 = f32[3072,512]{1,0:T(8,128)} fusion(f32[3072,512]{1,0:T(8,128)} %get-tuple-element.231, s32[512]{0:T(512)S(1)} %get-tuple-element.220, pred[]{:T(512)S(6)} %compare.23, bf16[512]{0:T(512)(128)(2,1)S(1)} %dynamic_slice.35, s32[512]{0:T(512)S(1)} %get-tuple-element.221), kind=kOutput, calls=%fused_computation.3.clone.1 | convolution fusion | flops 1617166336 | bytes 12588033 | tf_op jit(solution)/shard_map/while/body/eval_jaxpr/dot_general | solution.py:81
  103.5 0.1 dynamic_slice.35
  103.6 0.1 add_select_fusion.3
  103.7 7.5 %select_add_fusion.2 = f32[3072,512]{1,0:T(8,128)} fusion(f32[3072,512]{1,0:T(8,128)} %get-tuple-element.231, s32[512]{0:T(512)S(1)} %get-tuple-element.220, pred[]{:T(512)S(6)} %compare.23, bf16[512]{0:T(512)(128)(2,1)S(1)} %dynamic_slice.35, s32[512]{0:T(512)S(1)} %get-tuple-element.221), kind=kOutput, calls=%fused_computation.3.clone.1 | convolution fusion | flops 1617166336 | bytes 12588033 | tf_op jit(solution)/shard_map/while/body/eval_jaxpr/dot_general | solution.py:81
  111.2 0.1 dynamic_slice.35
  111.3 0.1 add_select_fusion.3
  111.4 7.5 %select_add_fusion.2 = f32[3072,512]{1,0:T(8,128)} fusion(f32[3072,512]{1,0:T(8,128)} %get-tuple-element.231, s32[512]{0:T(512)S(1)} %get-tuple-element.220, pred[]{:T(512)S(6)} %compare.23, bf16[512]{0:T(512)(128)(2,1)S(1)} %dynamic_slice.35, s32[512]{0:T(512)S(1)} %get-tuple-element.221), kind=kOutput, calls=%fused_computation.3.clone.1 | convolution fusion | flops 1617166336 | bytes 12588033 | tf_op jit(solution)/shard_map/while/body/eval_jaxpr/dot_general | solution.py:81
  118.9 0.1 dynamic_slice.35
  119.0 0.1 add_select_fusion.3
  119.0 7.5 %select_add_fusion.2 = f32[3072,512]{1,0:T(8,128)} fusion(f32[3072,512]{1,0:T(8,128)} %get-tuple-element.231, s32[512]{0:T(512)S(1)} %get-tuple-element.220, pred[]{:T(512)S(6)} %compare.23, bf16[512]{0:T(512)(128)(2,1)S(1)} %dynamic_slice.35, s32[512]{0:T(512)S(1)} %get-tuple-element.221), kind=kOutput, calls=%fused_computation.3.clone.1 | convolution fusion | flops 1617166336 | bytes 12588033 | tf_op jit(solution)/shard_map/while/body/eval_jaxpr/dot_general | solution.py:81
  126.6 0.1 dynamic_slice.35
  126.6 0.1 add_select_fusion.3
  126.7 7.5 %select_add_fusion.2 = f32[3072,512]{1,0:T(8,128)} fusion(f32[3072,512]{1,0:T(8,128)} %get-tuple-element.231, s32[512]{0:T(512)S(1)} %get-tuple-element.220, pred[]{:T(512)S(6)} %compare.23, bf16[512]{0:T(512)(128)(2,1)S(1)} %dynamic_slice.35, s32[512]{0:T(512)S(1)} %get-tuple-element.221), kind=kOutput, calls=%fused_computation.3.clone.1 | convolution fusion | flops 1617166336 | bytes 12588033 | tf_op jit(solution)/shard_map/while/body/eval_jaxpr/dot_general | solution.py:81
  134.2 0.1 dynamic_slice.35
  134.3 0.1 add_select_fusion.3
  134.4 7.5 %select_add_fusion.2 = f32[3072,512]{1,0:T(8,128)} fusion(f32[3072,512]{1,0:T(8,128)} %get-tuple-element.231, s32[512]{0:T(512)S(1)} %get-tuple-element.220, pred[]{:T(512)S(6)} %compare.23, bf16[512]{0:T(512)(128)(2,1)S(1)} %dynamic_slice.35, s32[512]{0:T(512)S(1)} %get-tuple-element.221), kind=kOutput, calls=%fused_computation.3.clone.1 | convolution fusion | flops 1617166336 | bytes 12588033 | tf_op jit(solution)/shard_map/while/body/eval_jaxpr/dot_general | solution.py:81
  141.9 0.1 dynamic_slice.35
  142.0 0.1 add_select_fusion.3
  142.1 7.5 %select_add_fusion.2 = f32[3072,512]{1,0:T(8,128)} fusion(f32[3072,512]{1,0:T(8,128)} %get-tuple-element.231, s32[512]{0:T(512)S(1)} %get-tuple-element.220, pred[]{:T(512)S(6)} %compare.23, bf16[512]{0:T(512)(128)(2,1)S(1)} %dynamic_slice.35, s32[512]{0:T(512)S(1)} %get-tuple-element.221), kind=kOutput, calls=%fused_computation.3.clone.1 | convolution fusion | flops 1617166336 | bytes 12588033 | tf_op jit(solution)/shard_map/while/body/eval_jaxpr/dot_general | solution.py:81
  149.6 2.7 %slice.32 = bf16[1024,512]{1,0:T(8,128)(2,1)} slice(f32[3072,512]{1,0:T(8,128)} %get-tuple-element.159), slice={[2048:3072], [0:512]} | slice | bytes 2097152 | tf_op jit(solution)/shard_map/slice | solution.py:111
  152.3 3.7 %all-to-all-start.3 = ((bf16[16,64,512]{2,1,0:T(8,128)(2,1)}), bf16[16,64,512]{2,1,0:T(8,128)(2,1)S(1)}, u32[]{:S(2)}, u32[]{:S(2)}) async-start(bf16[16,64,512]{2,1,0:T(8,128)(2,1)} %bitcast.19), calls=%async_computation.3 | async-start | bytes 2097152 | tf_op jit(solution)/shard_map/all_to_all | solution.py:54
  156.0 2.7 %slice_multiply_fusion = f32[2048,512]{1,0:T(8,128)S(1)} fusion(f32[3072,512]{1,0:T(8,128)} %get-tuple-element.159, f32[]{:T(128)S(6)} %div.35), kind=kLoop, calls=%fused_computation.20 | loop fusion | flops 1048576 | bytes 8388612 | tf_op jit(solution)/shard_map/mul | solution.py:116
  158.7 2.7 %maximum_log_fusion = f32[4,512,512]{2,1,0:T(8,128)} fusion(f32[4,512,512]{2,1,0:T(8,128)S(1)} %bitcast.56, f32[4,512]{1,0:T(4,128)S(1)} %fusion.17, f32[4,512]{1,0:T(4,128)S(1)} %fusion.16), kind=kLoop, calls=%fused_computation.19 | loop fusion | flops 3145728 | bytes 8404992 | tf_op jit(solution)/shard_map/log | solution.py:115
  161.3 12.3 %all-to-all-done.3 = bf16[16,64,512]{2,1,0:T(8,128)(2,1)S(1)} async-done(((bf16[16,64,512]{2,1,0:T(8,128)(2,1)}), bf16[16,64,512]{2,1,0:T(8,128)(2,1)S(1)}, u32[]{:S(2)}, u32[]{:S(2)}) %all-to-all-start.3) | async-done | bytes 1048608 | tf_op jit(solution)/shard_map/all_to_all | solution.py:54
  173.7 0.1 convert_reduce_fusion
  173.8 0.9 fusion.14
  (9 shorter events, 0.1 us)
Async XLA Ops:
  2.0 57.6 %all-to-all-start.1 = ((s32[128,1,1,1]{3,2,1,0:T(1,128)}), s32[128,1,1,1]{3,2,1,0:T(1,128)S(1)}, u32[]{:S(2)}, u32[]{:S(2)}) async-start(s32[128,1,1,1]{3,2,1,0:T(1,128)} %copy.16), calls=%async_computation.1 | async-start | bytes 131072 | tf_op jit(solution)/shard_map/all_to_all | solution.py:33
  59.6 17.2 %all-to-all-start.2 = ((bf16[128,1,1,32]{3,2,1,0:T(2,128)(2,1)}), bf16[128,1,1,32]{3,2,1,0:T(2,128)(2,1)S(1)}, u32[]{:S(2)}, u32[]{:S(2)}) async-start(bf16[128,1,1,32]{3,2,1,0:T(2,128)(2,1)} %reshape_transpose_transpose_reshape_reshape_reshape.12), calls=%async_computation.2 | async-start | bytes 131072 | tf_op jit(solution)/shard_map/all_to_all | solution.py:33
  76.8 14.0 %all-to-all-start = ((s32[128,1,1,32]{3,2,1,0:T(1,128)}), s32[128,1,1,32]{3,2,1,0:T(1,128)S(1)}, u32[]{:S(2)}, u32[]{:S(2)}) async-start(s32[128,1,1,32]{3,2,1,0:T(1,128)} %bitcast.2), calls=%async_computation | async-start | bytes 131072 | tf_op jit(solution)/shard_map/all_to_all | solution.py:33
  152.3 21.3 %all-to-all-start.3 = ((bf16[16,64,512]{2,1,0:T(8,128)(2,1)}), bf16[16,64,512]{2,1,0:T(8,128)(2,1)S(1)}, u32[]{:S(2)}, u32[]{:S(2)}) async-start(bf16[16,64,512]{2,1,0:T(8,128)(2,1)} %bitcast.19), calls=%async_computation.3 | async-start | bytes 2097152 | tf_op jit(solution)/shard_map/all_to_all | solution.py:54
where the time goes:
time: 176 us; the launch traced here: 175 us
  matrix products  59.2 us (34%)
  blocking collectives  37.8 us (21%)
  waiting for transfers between devices  28.4 us (16%)
  starting transfers between devices  27.1 us (15%)
  other arithmetic  11.5 us (7%)
  local copies, waits for them, and re-layouts  9.26 us (5%)
    dot_general x8, matrix products, step_block(): lax.dot_general(left_side, right_side, (((0,), (0,)), ((), ())), preferre...  57.3 us
    all_gather x4, blocking collectives, stacked_from(): blocks = lax.all_gather(blocks, axes[k], axis=0, tiled=True)  37.8 us
    all_to_all x3, starting transfers between devices, one_exchange(): lax.all_to_all(blocks, axis, split_axis=0, concat_axis=0, tiled=True)  23.5 us
    all_to_all x3, waiting for transfers between devices, one_exchange(): lax.all_to_all(blocks, axis, split_axis=0, concat_axis=0, tiled=True)  16.1 us
    all_to_all x1, waiting for transfers between devices, sum_at_owner(): blocks = lax.all_to_all(cut_along(x, dim, size), axis, 0, 0, tiled=True)  12.3 us
    all_to_all x1, starting transfers between devices, sum_at_owner(): blocks = lax.all_to_all(cut_along(x, dim, size), axis, 0, 0, tiled=True)  3.65 us
  transfers between devices with their start and end apart: 4, of which 3 were waited for; matrix products, arithmetic and copies ran while one was open for 9% of the time, Pallas kernels for 0%

commit v1 on v0

--- a/solution.py
+++ b/solution.py
@@ -38,7 +38,10 @@
 def stacked_from(x, axes, order):
     blocks = x[None]
     for k in order:
-        blocks = lax.all_gather(blocks, axes[k], axis=0, tiled=True)
+        count = lax.axis_size(axes[k])
+        pieces = jnp.stack([blocks for _ in range(count)])
+        pieces = lax.all_to_all(pieces, axes[k], split_axis=0, concat_axis=0)
+        blocks = jnp.concatenate(pieces, axis=0)
     block = [lax.axis_size(axes[k]) for k in reversed(order)]
     blocks = blocks.reshape(*block, *x.shape)
     turned = sorted(range(len(order)), key=lambda place: order[len(order) - 1 - place])

time: 176 us -> 166 us (0.943)
  blocking collectives: 37.8 us -> 3.94 us
  waiting for transfers between devices: 28.4 us -> 40.2 us
  starting transfers between devices: 27.1 us -> 36.6 us
  local copies, waits for them, and re-layouts: 9.26 us -> 12 us
    all_gather x4 -> x0, blocking collectives: 37.8 us -> none  [stacked_from(): blocks = lax.all_gather(blocks, axes[k], axis=0, tiled=True)]
    all_to_all x0 -> x3, starting transfers between devices: none -> 9.84 us  [stacked_from(): pieces = lax.all_to_all(pieces, axes[k], split_axis=0, concat_axis=0)]
    all_to_all x0 -> x3, waiting for transfers between devices: none -> 8.14 us  [stacked_from(): pieces = lax.all_to_all(pieces, axes[k], split_axis=0, concat_axis=0)]
    all_to_all x3, waiting for transfers between devices: 16.1 us -> 22.1 us  [one_exchange(): lax.all_to_all(blocks, axis, split_axis=0, concat_axis=0, tiled=True)]
    all_to_all x0 -> x1, blocking collectives: none -> 3.94 us  [stacked_from(): pieces = lax.all_to_all(pieces, axes[k], split_axis=0, concat_axis=0)]
    another operation x0 -> x4, local copies, waits for them, and re-layouts: none -> 2.59 us  [stacked_from(): pieces = jnp.stack([blocks for _ in range(count)])]
    all_to_all x1, waiting for transfers between devices: 12.3 us -> 10 us  [sum_at_owner(): blocks = lax.all_to_all(cut_along(x, dim, size), axis, 0, 0, tiled=True)]
    all_to_all x3, starting transfers between devices: 23.5 us -> 21.3 us  [one_exchange(): lax.all_to_all(blocks, axis, split_axis=0, concat_axis=0, tiled=True)]
  transfers between devices with their start and end apart: 4 -> 7, of which waited for: 3 -> 6; matrix products, arithmetic and copies ran while one was open for 9% -> 47% of each run, Pallas kernels for 0% -> 0%
where the time goes in v1:
time: 166 us; the launch traced here: 165 us
  matrix products  59.2 us (36%)
  waiting for transfers between devices  40.2 us (24%)
  starting transfers between devices  36.6 us (22%)
  local copies, waits for them, and re-layouts  12 us (7%)
  other arithmetic  11.5 us (7%)
  blocking collectives  3.94 us (2%)
    dot_general x8, matrix products, step_block(): lax.dot_general(left_side, right_side, (((0,), (0,)), ((), ())), preferre...  57.3 us
    all_to_all x3, waiting for transfers between devices, one_exchange(): lax.all_to_all(blocks, axis, split_axis=0, concat_axis=0, tiled=True)  22.1 us
    all_to_all x3, starting transfers between devices, one_exchange(): lax.all_to_all(blocks, axis, split_axis=0, concat_axis=0, tiled=True)  21.3 us
    all_to_all x1, waiting for transfers between devices, sum_at_owner(): blocks = lax.all_to_all(cut_along(x, dim, size), axis, 0, 0, tiled=True)  10 us
    all_to_all x3, starting transfers between devices, stacked_from(): pieces = lax.all_to_all(pieces, axes[k], split_axis=0, concat_axis=0)  9.84 us
    all_to_all x3, waiting for transfers between devices, stacked_from(): pieces = lax.all_to_all(pieces, axes[k], split_axis=0, concat_axis=0)  8.14 us
    all_to_all x1, starting transfers between devices, sum_at_owner(): blocks = lax.all_to_all(cut_along(x, dim, size), axis, 0, 0, tiled=True)  5.45 us
    all_to_all x1, blocking collectives, stacked_from(): pieces = lax.all_to_all(pieces, axes[k], split_axis=0, concat_axis=0)  3.94 us
  transfers between devices with their start and end apart: 7, of which 6 were waited for; matrix products, arithmetic and copies ran while one was open for 47% of the time, Pallas kernels for 0%

profile of v1, /device:TPU:0, one launch (start us, length us, event | category | flops | bytes accessed | tf_op | source)
XLA Modules:
  0.0 164.8 jit_solution(16265589778900287642)
XLA Ops:
  0.6 1.4 copy.20
  2.0 11.2 %all-to-all-start.5 = ((s32[128,1,1,1]{3,2,1,0:T(1,128)}), s32[128,1,1,1]{3,2,1,0:T(1,128)S(1)}, u32[]{:S(2)}, u32[]{:S(2)}) async-start(s32[128,1,1,1]{3,2,1,0:T(1,128)} %copy.20), calls=%async_computation.5 | async-start | bytes 131072 | tf_op jit(solution)/shard_map/all_to_all | solution.py:33
  13.2 0.8 slice_bitcast_fusion.1
  14.0 8.7 %all-to-all-done.5 = s32[128,1,1,1]{3,2,1,0:T(1,128)S(1)} async-done(((s32[128,1,1,1]{3,2,1,0:T(1,128)}), s32[128,1,1,1]{3,2,1,0:T(1,128)S(1)}, u32[]{:S(2)}, u32[]{:S(2)}) %all-to-all-start.5) | async-done | bytes 544 | tf_op jit(solution)/shard_map/all_to_all | solution.py:33
  22.6 1.3 stack.12
  23.9 3.2 %all-to-all-start = ((f32[4,1,1,512]{3,2,1,0:T(1,128)}), f32[4,1,1,512]{3,2,1,0:T(1,128)S(1)}, u32[]{:S(2)}, u32[]{:S(2)}) async-start(f32[4,1,1,512]{3,2,1,0:T(1,128)} %stack.12), calls=%async_computation | async-start | bytes 16384 | tf_op jit(solution)/shard_map/all_to_all | solution.py:43
  27.2 1.0 slice_reduce_fusion.1
  28.1 0.8 reduce.5
  28.9 0.7 reshape_transpose_transpose_reshape_reshape_reshape.12
  29.6 2.8 %all-to-all-done = f32[4,1,1,512]{3,2,1,0:T(1,128)S(1)} async-done(((f32[4,1,1,512]{3,2,1,0:T(1,128)}), f32[4,1,1,512]{3,2,1,0:T(1,128)S(1)}, u32[]{:S(2)}, u32[]{:S(2)}) %all-to-all-start) | async-done | bytes 8224 | tf_op jit(solution)/shard_map/all_to_all | solution.py:43
  32.5 4.6 %all-to-all-start.6 = ((bf16[128,1,1,32]{3,2,1,0:T(2,128)(2,1)}), bf16[128,1,1,32]{3,2,1,0:T(2,128)(2,1)S(1)}, u32[]{:S(2)}, u32[]{:S(2)}) async-start(bf16[128,1,1,32]{3,2,1,0:T(2,128)(2,1)} %reshape_transpose_transpose_reshape_reshape_reshape.12), calls=%async_computation.6 | async-start | bytes 131072 | tf_op jit(solution)/shard_map/all_to_all | solution.py:33
  37.1 0.5 broadcast.155
  37.6 1.4 reduce.12
  39.0 0.7 reshape_transpose_transpose_reshape_reshape_reshape.9
  39.7 2.3 %reduce.4 = s32[128]{0:T(128)S(1)} reduce(s32[128,1,1,1]{3,2,1,0:T(1,128)S(1)} %all-to-all-done.5, s32[]{:T(128)} %constant.122.clone.1), dimensions={1,2,3}, to_apply=%all_to_all.29.reduce_sub_computation | reduce | bytes 1028 | tf_op jit(solution)/shard_map/all_to_all | solution.py:33
  42.1 0.1 reshape.101
  42.1 0.1 lt.51
  42.2 4.3 %all-to-all-done.6 = bf16[128,1,1,32]{3,2,1,0:T(2,128)(2,1)S(1)} async-done(((bf16[128,1,1,32]{3,2,1,0:T(2,128)(2,1)}), bf16[128,1,1,32]{3,2,1,0:T(2,128)(2,1)S(1)}, u32[]{:S(2)}, u32[]{:S(2)}) %all-to-all-start.6) | async-done | bytes 8224 | tf_op jit(solution)/shard_map/all_to_all | solution.py:33
  46.5 5.5 %all-to-all-start.4 = ((s32[128,1,1,32]{3,2,1,0:T(1,128)}), s32[128,1,1,32]{3,2,1,0:T(1,128)S(1)}, u32[]{:S(2)}, u32[]{:S(2)}) async-start(s32[128,1,1,32]{3,2,1,0:T(1,128)} %bitcast.2), calls=%async_computation.4 | async-start | bytes 131072 | tf_op jit(solution)/shard_map/all_to_all | solution.py:33
  52.0 0.1 iota_compare_fusion.3
  52.1 0.1 lt.54
  52.2 0.1 reshape_reshape.10
  52.3 9.1 %all-to-all-done.4 = s32[128,1,1,32]{3,2,1,0:T(1,128)S(1)} async-done(((s32[128,1,1,32]{3,2,1,0:T(1,128)}), s32[128,1,1,32]{3,2,1,0:T(1,128)S(1)}, u32[]{:S(2)}, u32[]{:S(2)}) %all-to-all-start.4) | async-done | bytes 16416 | tf_op jit(solution)/shard_map/all_to_all | solution.py:33
  61.4 0.6 stack.13
  62.1 3.3 %all-to-all-start.1 = ((f32[4,4,1,512]{3,1,2,0:T(4,128)}), f32[4,4,1,512]{3,1,2,0:T(4,128)S(1)}, u32[]{:S(2)}, u32[]{:S(2)}) async-start(f32[4,4,1,512]{3,1,2,0:T(4,128)} %stack.13), calls=%async_computation.1 | async-start | bytes 65536 | tf_op jit(solution)/shard_map/all_to_all | solution.py:43
  65.4 0.1 reshape_reshape_reshape.3
  65.4 5.3 %all-to-all-done.1 = f32[4,4,1,512]{3,1,2,0:T(4,128)S(1)} async-done(((f32[4,4,1,512]{3,1,2,0:T(4,128)}), f32[4,4,1,512]{3,1,2,0:T(4,128)S(1)}, u32[]{:S(2)}, u32[]{:S(2)}) %all-to-all-start.1) | async-done | bytes 32800 | tf_op jit(solution)/shard_map/all_to_all | solution.py:43
  70.8 0.7 stack.14
  71.4 3.3 %all-to-all-start.2 = ((f32[4,16,1,512]{3,1,2,0:T(8,128)}), f32[4,16,1,512]{3,1,2,0:T(8,128)S(1)}, u32[]{:S(2)}, u32[]{:S(2)}) async-start(f32[4,16,1,512]{3,1,2,0:T(8,128)} %stack.14), calls=%async_computation.2 | async-start | bytes 262144 | tf_op jit(solution)/shard_map/all_to_all | solution.py:43
  74.8 58.7 %while.16 = (s32[]{:T(128)}, f32[3072,512]{1,0:T(8,128)}, s32[4096]{0:T(1024)S(1)}, bf16[4096]{0:T(1024)(128)(2,1)S(1)}, s32[]{:T(128)}, /*index=5*/s32[]{:T(128)}, s32[]{:T(128)}, s32[]{:T(128)}) while((s32[]{:T(128)}, f32[3072,512]{1,0:T(8,128)}, s32[4096]{0:T(1024)S(1)}, bf16[4096]{0:T(1024)(128)(2,1)S(1)}, s32[]{:T(128)}, ...), condition=%wide.region_2.3_spmd.clone, body=%wide.region_1.2_spmd.clone.sunk | while | flops 1617176064 | bytes 12596381 | solution.py:88
  74.8 0.1 dynamic_slice.35
  74.9 0.1 add_select_fusion.3
  75.0 4.7 %select_add_fusion.2 = f32[3072,512]{1,0:T(8,128)} fusion(f32[3072,512]{1,0:T(8,128)} %get-tuple-element.231, s32[512]{0:T(512)S(1)} %get-tuple-element.220, pred[]{:T(512)S(6)} %compare.23, bf16[512]{0:T(512)(128)(2,1)S(1)} %dynamic_slice.35, s32[512]{0:T(512)S(1)} %get-tuple-element.221), kind=kOutput, calls=%fused_computation.3.clone.1 | convolution fusion | flops 1617166336 | bytes 12588033 | tf_op jit(solution)/shard_map/while/body/eval_jaxpr/dot_general | solution.py:84
  79.8 0.1 add_select_fusion.3
  79.9 7.5 %select_add_fusion.2 = f32[3072,512]{1,0:T(8,128)} fusion(f32[3072,512]{1,0:T(8,128)} %get-tuple-element.231, s32[512]{0:T(512)S(1)} %get-tuple-element.220, pred[]{:T(512)S(6)} %compare.23, bf16[512]{0:T(512)(128)(2,1)S(1)} %dynamic_slice.35, s32[512]{0:T(512)S(1)} %get-tuple-element.221), kind=kOutput, calls=%fused_computation.3.clone.1 | convolution fusion | flops 1617166336 | bytes 12588033 | tf_op jit(solution)/shard_map/while/body/eval_jaxpr/dot_general | solution.py:84
  87.4 0.1 add_select_fusion.3
  87.5 7.5 %select_add_fusion.2 = f32[3072,512]{1,0:T(8,128)} fusion(f32[3072,512]{1,0:T(8,128)} %get-tuple-element.231, s32[512]{0:T(512)S(1)} %get-tuple-element.220, pred[]{:T(512)S(6)} %compare.23, bf16[512]{0:T(512)(128)(2,1)S(1)} %dynamic_slice.35, s32[512]{0:T(512)S(1)} %get-tuple-element.221), kind=kOutput, calls=%fused_computation.3.clone.1 | convolution fusion | flops 1617166336 | bytes 12588033 | tf_op jit(solution)/shard_map/while/body/eval_jaxpr/dot_general | solution.py:84
  95.1 0.1 add_select_fusion.3
  95.2 7.5 %select_add_fusion.2 = f32[3072,512]{1,0:T(8,128)} fusion(f32[3072,512]{1,0:T(8,128)} %get-tuple-element.231, s32[512]{0:T(512)S(1)} %get-tuple-element.220, pred[]{:T(512)S(6)} %compare.23, bf16[512]{0:T(512)(128)(2,1)S(1)} %dynamic_slice.35, s32[512]{0:T(512)S(1)} %get-tuple-element.221), kind=kOutput, calls=%fused_computation.3.clone.1 | convolution fusion | flops 1617166336 | bytes 12588033 | tf_op jit(solution)/shard_map/while/body/eval_jaxpr/dot_general | solution.py:84
  102.8 0.1 add_select_fusion.3
  102.9 7.5 %select_add_fusion.2 = f32[3072,512]{1,0:T(8,128)} fusion(f32[3072,512]{1,0:T(8,128)} %get-tuple-element.231, s32[512]{0:T(512)S(1)} %get-tuple-element.220, pred[]{:T(512)S(6)} %compare.23, bf16[512]{0:T(512)(128)(2,1)S(1)} %dynamic_slice.35, s32[512]{0:T(512)S(1)} %get-tuple-element.221), kind=kOutput, calls=%fused_computation.3.clone.1 | convolution fusion | flops 1617166336 | bytes 12588033 | tf_op jit(solution)/shard_map/while/body/eval_jaxpr/dot_general | solution.py:84
  110.5 0.1 add_select_fusion.3
  110.6 7.5 %select_add_fusion.2 = f32[3072,512]{1,0:T(8,128)} fusion(f32[3072,512]{1,0:T(8,128)} %get-tuple-element.231, s32[512]{0:T(512)S(1)} %get-tuple-element.220, pred[]{:T(512)S(6)} %compare.23, bf16[512]{0:T(512)(128)(2,1)S(1)} %dynamic_slice.35, s32[512]{0:T(512)S(1)} %get-tuple-element.221), kind=kOutput, calls=%fused_computation.3.clone.1 | convolution fusion | flops 1617166336 | bytes 12588033 | tf_op jit(solution)/shard_map/while/body/eval_jaxpr/dot_general | solution.py:84
  118.1 0.1 add_select_fusion.3
  118.2 7.5 %select_add_fusion.2 = f32[3072,512]{1,0:T(8,128)} fusion(f32[3072,512]{1,0:T(8,128)} %get-tuple-element.231, s32[512]{0:T(512)S(1)} %get-tuple-element.220, pred[]{:T(512)S(6)} %compare.23, bf16[512]{0:T(512)(128)(2,1)S(1)} %dynamic_slice.35, s32[512]{0:T(512)S(1)} %get-tuple-element.221), kind=kOutput, calls=%fused_computation.3.clone.1 | convolution fusion | flops 1617166336 | bytes 12588033 | tf_op jit(solution)/shard_map/while/body/eval_jaxpr/dot_general | solution.py:84
  125.8 0.1 add_select_fusion.3
  125.9 7.5 %select_add_fusion.2 = f32[3072,512]{1,0:T(8,128)} fusion(f32[3072,512]{1,0:T(8,128)} %get-tuple-element.231, s32[512]{0:T(512)S(1)} %get-tuple-element.220, pred[]{:T(512)S(6)} %compare.23, bf16[512]{0:T(512)(128)(2,1)S(1)} %dynamic_slice.35, s32[512]{0:T(512)S(1)} %get-tuple-element.221), kind=kOutput, calls=%fused_computation.3.clone.1 | convolution fusion | flops 1617166336 | bytes 12588033 | tf_op jit(solution)/shard_map/while/body/eval_jaxpr/dot_general | solution.py:84
  133.4 2.7 %slice.32 = bf16[1024,512]{1,0:T(8,128)(2,1)} slice(f32[3072,512]{1,0:T(8,128)} %get-tuple-element.159), slice={[2048:3072], [0:512]} | slice | bytes 2097152 | tf_op jit(solution)/shard_map/slice | solution.py:114
  136.2 3.9 %all_to_all.40 = f32[2,64,1,512]{3,1,2,0:T(8,128)S(1)} all-to-all(f32[2,64,1,512]{3,1,2,0:T(8,128)S(1)} %pad_maximum_fusion), channel_id=1, replica_groups=mesh['row_0'=4,'row_1'=2,'col_0'=4,'col_1'=4] {'row_1'}, dimensions={0} | all-to-all | bytes 524288 | tf_op jit(solution)/shard_map/all_to_all | solution.py:43
  140.1 5.5 %all-to-all-start.7 = ((bf16[16,64,512]{2,1,0:T(8,128)(2,1)}), bf16[16,64,512]{2,1,0:T(8,128)(2,1)S(1)}, u32[]{:S(2)}, u32[]{:S(2)}) async-start(bf16[16,64,512]{2,1,0:T(8,128)(2,1)} %bitcast.20), calls=%async_computation.7 | async-start | bytes 2097152 | tf_op jit(solution)/shard_map/all_to_all | solution.py:57
  145.6 0.2 copy.22
  145.8 0.2 copy.23
  146.0 0.1 reshape_reshape.12
  146.1 0.2 fusion.18
  146.3 0.2 fusion.17
  146.5 0.7 reduce_sum.18
  147.8 2.7 %slice_multiply_fusion = f32[2048,512]{1,0:T(8,128)S(1)} fusion(f32[3072,512]{1,0:T(8,128)} %get-tuple-element.159, f32[]{:T(128)S(6)} %div.35), kind=kLoop, calls=%fused_computation.20 | loop fusion | flops 1048576 | bytes 8388612 | tf_op jit(solution)/shard_map/mul | solution.py:119
  150.5 0.2 convolution_bitcast_fusion
  150.7 0.1 dynamic_slice.23
  150.8 0.2 fusion.16
  151.0 2.6 %maximum_log_fusion = f32[4,512,512]{2,1,0:T(8,128)} fusion(f32[4,512,512]{2,1,0:T(8,128)S(1)} %bitcast.61, f32[4,512]{1,0:T(4,128)S(1)} %fusion.17, f32[4,512]{1,0:T(4,128)S(1)} %fusion.16), kind=kLoop, calls=%fused_computation.19 | loop fusion | flops 3145728 | bytes 8404992 | tf_op jit(solution)/shard_map/log | solution.py:118
  153.7 10.0 %all-to-all-done.7 = bf16[16,64,512]{2,1,0:T(8,128)(2,1)S(1)} async-done(((bf16[16,64,512]{2,1,0:T(8,128)(2,1)}), bf16[16,64,512]{2,1,0:T(8,128)(2,1)S(1)}, u32[]{:S(2)}, u32[]{:S(2)}) %all-to-all-start.7) | async-done | bytes 1048608 | tf_op jit(solution)/shard_map/all_to_all | solution.py:57
  163.7 0.1 convert_reduce_fusion
  163.9 0.9 fusion.14
  (16 shorter events, 0.6 us)
Async XLA Ops:
  2.0 20.6 %all-to-all-start.5 = ((s32[128,1,1,1]{3,2,1,0:T(1,128)}), s32[128,1,1,1]{3,2,1,0:T(1,128)S(1)}, u32[]{:S(2)}, u32[]{:S(2)}) async-start(s32[128,1,1,1]{3,2,1,0:T(1,128)} %copy.20), calls=%async_computation.5 | async-start | bytes 131072 | tf_op jit(solution)/shard_map/all_to_all | solution.py:33
  23.9 8.5 %all-to-all-start = ((f32[4,1,1,512]{3,2,1,0:T(1,128)}), f32[4,1,1,512]{3,2,1,0:T(1,128)S(1)}, u32[]{:S(2)}, u32[]{:S(2)}) async-start(f32[4,1,1,512]{3,2,1,0:T(1,128)} %stack.12), calls=%async_computation | async-start | bytes 16384 | tf_op jit(solution)/shard_map/all_to_all | solution.py:43
  32.5 14.0 %all-to-all-start.6 = ((bf16[128,1,1,32]{3,2,1,0:T(2,128)(2,1)}), bf16[128,1,1,32]{3,2,1,0:T(2,128)(2,1)S(1)}, u32[]{:S(2)}, u32[]{:S(2)}) async-start(bf16[128,1,1,32]{3,2,1,0:T(2,128)(2,1)} %reshape_transpose_transpose_reshape_reshape_reshape.12), calls=%async_computation.6 | async-start | bytes 131072 | tf_op jit(solution)/shard_map/all_to_all | solution.py:33
  46.5 15.0 %all-to-all-start.4 = ((s32[128,1,1,32]{3,2,1,0:T(1,128)}), s32[128,1,1,32]{3,2,1,0:T(1,128)S(1)}, u32[]{:S(2)}, u32[]{:S(2)}) async-start(s32[128,1,1,32]{3,2,1,0:T(1,128)} %bitcast.2), calls=%async_computation.4 | async-start | bytes 131072 | tf_op jit(solution)/shard_map/all_to_all | solution.py:33
  62.1 8.7 %all-to-all-start.1 = ((f32[4,4,1,512]{3,1,2,0:T(4,128)}), f32[4,4,1,512]{3,1,2,0:T(4,128)S(1)}, u32[]{:S(2)}, u32[]{:S(2)}) async-start(f32[4,4,1,512]{3,1,2,0:T(4,128)} %stack.13), calls=%async_computation.1 | async-start | bytes 65536 | tf_op jit(solution)/shard_map/all_to_all | solution.py:43
  71.4 64.7 %all-to-all-start.2 = ((f32[4,16,1,512]{3,1,2,0:T(8,128)}), f32[4,16,1,512]{3,1,2,0:T(8,128)S(1)}, u32[]{:S(2)}, u32[]{:S(2)}) async-start(f32[4,16,1,512]{3,1,2,0:T(8,128)} %stack.14), calls=%async_computation.2 | async-start | bytes 262144 | tf_op jit(solution)/shard_map/all_to_all | solution.py:43
  140.1 23.6 %all-to-all-start.7 = ((bf16[16,64,512]{2,1,0:T(8,128)(2,1)}), bf16[16,64,512]{2,1,0:T(8,128)(2,1)S(1)}, u32[]{:S(2)}, u32[]{:S(2)}) async-start(bf16[16,64,512]{2,1,0:T(8,128)(2,1)} %bitcast.20), calls=%async_computation.7 | async-start | bytes 2097152 | tf_op jit(solution)/shard_map/all_to_all | solution.py:57
